TPU v7x, 32 devices: a whole 2x2x4 slice. The times are simulated.
32 devices in a mesh: row: 8 (over z, core), col: 4 (over y, x).
Axes of the slice: x: 2, y: 2, z: 4, core: 2. Of those that a mesh axis runs over, the one named last changes fastest.
Arguments:
- tokens: bfloat16 [512, 4096], P(None, 'col'), may hold values from -6 to 6
- w_gate: bfloat16 [4096, 10240], P('col', 'row'), may hold values from -0.09375 to 0.09375
- w_up: bfloat16 [4096, 10240], P('col', 'row'), may hold values from -0.09375 to 0.09375
- w_down: bfloat16 [10240, 4096], P('row', 'col'), may hold values from -0.0625 to 0.0625
Outputs:
- result: bfloat16 [512, 4096], P('row', 'col')
All inputs are finite; a program needn't handle non-finite values.
Results may differ from a plain program's by a relative error of at most 0.025.
Values may be sent and summed in bfloat16 or wider, within the bound.
A program may use at most 64 MiB of HBM per device.

v0:
```python
import functools

import jax
import jax.numpy as jnp
from jax import lax
from jax.experimental import pallas as pl
from jax.experimental.pallas import tpu as pltpu
from jax.sharding import PartitionSpec as P

MESH = pl.DeviceIdType.MESH
PIECE = 8
TILE = 256


def activate(pre_gate, pre_up):
    return (jax.nn.gelu(pre_gate, approximate=True) * pre_up).astype(jnp.bfloat16)


def plain(tokens, w_gate, w_up, w_down):
    joined = jnp.concatenate([w_gate, w_up], axis=1)
    hidden_width = w_gate.shape[1]
    summed = lax.psum_scatter(
        jnp.dot(tokens, joined, preferred_element_type=jnp.float32).astype(jnp.bfloat16),
        "col",
        scatter_dimension=0,
        tiled=True,
    ).astype(jnp.float32)
    hidden = activate(summed[:, :hidden_width], summed[:, hidden_width:])
    hidden_all = lax.all_gather(hidden, "col", axis=0, tiled=True)
    result = lax.psum_scatter(
        jnp.dot(hidden_all, w_down, preferred_element_type=jnp.float32),
        "row",
        scatter_dimension=0,
        tiled=True,
    )
    return result.astype(jnp.bfloat16)


def chunk_rows(per_row):
    units = per_row // PIECE
    sizes = [1, 1, 2, 2, 1, 1] if units % 8 == 0 else [1] * units
    return [size * per_row // sum(sizes) for size in sizes]


def kernel(
    n_row, sizes, tok_hbm, wg_hbm, wu_hbm, wd_hbm, out_hbm,
    tok, w1, wd, s1, own, r1, s2, r2, hid, part, part16, c1r, c2s, c2r, out_ref,
    load_sem, send1, recv1, send2, recv2, send3, recv3, send4, recv4, send5, recv5, send6, recv6, store_sem,
):
    row, col = lax.axis_index("row"), lax.axis_index("col")
    y, x = col // 2, col % 2
    z, core = row // 2, row % 2
    n_z = n_row // 2
    chunks = len(sizes)
    spans = [pl.ds(sum(sizes[:i]), sizes[i]) for i in range(chunks)]
    half = w1.shape[2] // 2
    x_peer = (row, 2 * y + 1 - x)
    y_peer = (row, 2 * (1 - y) + x)
    core_peer = (2 * z + 1 - core, col)
    upper = 2 * z // n_z

    def z_order(k):
        down = n_z - 1 - k - (z + k + 1) // n_z
        up = k + (k + n_z - z) // n_z
        return down * (1 - upper) + up * upper

    z_others = [z_order(k) for k in range(n_z - 1)]
    z_peers = [(2 * other + core, col) for other in z_others]
    first_peer, second_peer = (x_peer, y_peer), (y_peer, x_peer)
    first_at, second_at = (x, y), (y, x)

    loads = [pltpu.make_async_copy(tok_hbm, tok, load_sem.at[0])]
    for mode in range(2):
        for k, w_hbm in enumerate((wg_hbm, wu_hbm)):
            loads.append(pltpu.make_async_copy(
                w_hbm.at[:, pl.ds(mode * half, half)],
                w1.at[mode, :, pl.ds(k * half, half)],
                load_sem.at[1 + 2 * mode + k],
            ))
    loads.append(pltpu.make_async_copy(wd_hbm, wd, load_sem.at[5]))
    for load in loads[:3]:
        load.start()

    barrier = pltpu.get_barrier_semaphore()
    peers = [x_peer, y_peer, core_peer] + z_peers
    for peer in peers:
        pl.semaphore_signal(barrier, inc=1, device_id=peer, device_id_type=MESH)

    def remote(src, dst, send_sem, recv_sem, peer):
        return pltpu.make_async_remote_copy(
            src_ref=src, dst_ref=dst, send_sem=send_sem, recv_sem=recv_sem, device_id=peer, device_id_type=MESH)

    def copy_s1(m, i):
        return remote(s1.at[m, :, :, spans[i]], r1.at[m, :, :, spans[i]], send1.at[m, i], recv1.at[m, i], first_peer[m])

    def copy_s2(m, i):
        return remote(s2.at[m, :, spans[i]], r2.at[m, :, spans[i]], send2.at[m, i], recv2.at[m, i], second_peer[m])

    def copy_g1(m, i):
        ref = hid.at[m, first_at[m], second_at[m], :, spans[i]]
        return remote(ref, ref, send3.at[m, i], recv3.at[m, i], second_peer[m])

    def copy_g2(m, i):
        ref = hid.at[m, first_at[m], :, :, spans[i]]
        return remote(ref, ref, send4.at[m, i], recv4.at[m, i], first_peer[m])

    def copy_c1(i):
        return remote(part16.at[1 - core, :, spans[i]], c1r.at[:, spans[i]], send5.at[i], recv5.at[i], core_peer)

    def copy_c2(i, k, arriving=False):
        at = z_others[k] if arriving else z
        return remote(c2s.at[z_others[k], spans[i]], c2r.at[at, spans[i]], send6.at[i, k], recv6.at[i, at], z_peers[k])

    def store(i):
        return pltpu.make_async_copy(out_ref.at[spans[i]], out_hbm.at[spans[i]], store_sem.at[i])

    def product(m, mine, dst, low, high):
        at = first_at[m] if mine else 1 - first_at[m]
        rows = tok[:, at, :, low:high] if m == 0 else tok[at, :, :, low:high]
        shape = rows.shape[:-1]
        rows = rows.reshape(-1, rows.shape[-1])
        for t in range(w1.shape[2] // TILE):
            columns = slice(t * TILE, (t + 1) * TILE)
            out = jnp.dot(rows, w1[m, :, columns], preferred_element_type=jnp.float32)
            dst[m, :, :, low:high, columns] = out.astype(jnp.bfloat16).reshape(*shape, TILE)

    def f32(v):
        return v.astype(jnp.float32)

    def do_s1(i):
        for m in range(2):
            copy_s1(m, i).start()

    def do_s2(i):
        for m in range(2):
            copy_s1(m, i).wait_recv()
            at, span = 1 - second_at[m], spans[i]
            s2[m, :, span] = (f32(own[m, at, :, span]) + f32(r1[m, at, :, span])).astype(jnp.bfloat16)
            copy_s2(m, i).start()

    def do_g1(i):
        for m in range(2):
            copy_s2(m, i).wait_recv()
            at, span = second_at[m], spans[i]
            pre = f32(own[m, at, :, span]) + f32(r1[m, at, :, span]) + f32(r2[m, :, span])
            hid[m, first_at[m], at, :, span] = activate(pre[..., :half], pre[..., half:])
            copy_g1(m, i).start()

    def do_g2(i):
        for m in range(2):
            copy_g1(m, i).wait_recv()
            copy_g2(m, i).start()

    def do_c1(i):
        for m in range(2):
            copy_g2(m, i).wait_recv()
        span = spans[i]
        rows = n_row // 4 * sizes[i]
        quarters = [
            jnp.concatenate([hid[0, b, a, :, span].reshape(rows, half), hid[1, a, b, :, span].reshape(rows, half)], axis=1)
            for a in range(2) for b in range(2)
        ]
        hidden = jnp.concatenate(quarters, axis=0)
        for t in range(wd.shape[1] // TILE):
            columns = slice(t * TILE, (t + 1) * TILE)
            out = jnp.dot(hidden, wd[:, columns], preferred_element_type=jnp.float32)
            out = out.reshape(n_z, 2, sizes[i], TILE)
            for c in range(2):
                part[c, :, span, columns] = out[:, c]
                part16[c, :, span, columns] = out[:, c].astype(jnp.bfloat16)
        copy_c1(i).start()

    def do_c2(i):
        copy_c1(i).wait_recv()
        span = spans[i]
        c2s[:, span] = (part[core, :, span] + f32(c1r[:, span])).astype(jnp.bfloat16)
        for k in range(n_z - 1):
            copy_c2(i, k).start()

    def do_out(i):
        span = spans[i]
        total = part[core, z, span] + f32(c1r[z, span])
        for k in reversed(range(n_z - 1)):
            copy_c2(i, k, True).wait_recv()
            total = total + f32(c2r[z_others[k], span])
        out_ref[span] = total.astype(jnp.bfloat16)
        store(i).start()

    first, ahead = min(2, chunks), min(3, chunks)
    cut, end = sum(sizes[:first]), sum(sizes)
    loads[0].wait()
    for load in loads[3:]:
        load.start()
    for m in range(2):
        for load in loads[1 + 2 * m:3 + 2 * m]:
            load.wait()
        product(m, False, s1, 0, cut)
        if m == 0:
            pl.semaphore_wait(barrier, len(peers))
        for i in range(first):
            copy_s1(m, i).start()
    for m in range(2):
        if cut < end:
            product(m, False, s1, cut, end)
            for i in range(first, ahead):
                copy_s1(m, i).start()
    for m in range(2):
        product(m, True, own, 0, end)
    loads[5].wait()

    for k in range(chunks + 4):
        for stage, late in ((do_s2, 0), (do_g1, 1), (do_s1, -3), (do_g2, 2), (do_c2, 4), (do_c1, 3)):
            i = k - late
            if 0 <= i < chunks and (stage is not do_s1 or i >= ahead):
                stage(i)
    for i in range(chunks):
        do_out(i)

    for i in range(chunks):
        for m in range(2):
            for copy in (copy_s1, copy_s2, copy_g1, copy_g2):
                copy(m, i).wait_send()
        copy_c1(i).wait_send()
        for k in range(n_z - 1):
            copy_c2(i, k).wait_send()
        store(i).wait()


def fused(n_row, tokens, w_gate, w_up, w_down):
    n_tok, depth = tokens.shape
    width, features = w_down.shape
    per_row = n_tok // n_row
    sizes = chunk_rows(per_row)
    chunks = len(sizes)
    n_z, blocks, half = n_row // 2, n_row // 4, width // 2
    bf16, dma = jnp.bfloat16, pltpu.SemaphoreType.DMA
    pair = [dma((2, chunks))] * 8
    return pl.pallas_call(
        functools.partial(kernel, n_row, sizes),
        out_shape=jax.ShapeDtypeStruct((per_row, features), bf16),
        in_specs=[pl.BlockSpec(memory_space=pl.ANY)] * 4,
        out_specs=pl.BlockSpec(memory_space=pl.ANY),
        scratch_shapes=[
            pltpu.VMEM((2, 2, blocks, per_row, depth), bf16),
            pltpu.VMEM((2, depth, width), bf16),
            pltpu.VMEM((width, features), bf16),
            pltpu.VMEM((2, 2, blocks, per_row, width), bf16),
            pltpu.VMEM((2, 2, blocks, per_row, width), bf16),
            pltpu.VMEM((2, 2, blocks, per_row, width), bf16),
            pltpu.VMEM((2, blocks, per_row, width), bf16),
            pltpu.VMEM((2, blocks, per_row, width), bf16),
            pltpu.VMEM((2, 2, 2, blocks, per_row, half), bf16),
            pltpu.VMEM((2, n_z, per_row, features), jnp.float32),
            pltpu.VMEM((2, n_z, per_row, features), bf16),
            pltpu.VMEM((n_z, per_row, features), bf16),
            pltpu.VMEM((n_z, per_row, features), bf16),
            pltpu.VMEM((n_z, per_row, features), bf16),
            pltpu.VMEM((per_row, features), bf16),
            dma((6,)),
            *pair,
            dma((chunks,)), dma((chunks,)),
            dma((chunks, n_z - 1)), dma((chunks, n_z)), dma((chunks,)),
        ],
        compiler_params=pltpu.CompilerParams(
            collective_id=0, has_side_effects=True, vmem_limit_bytes=67043328
        ),
    )(tokens.reshape(2, 2, blocks, per_row, depth), w_gate, w_up, w_down)


def solution(mesh):
    n_row, n_col = mesh.shape["row"], mesh.shape["col"]

    def local(tokens, w_gate, w_up, w_down):
        width, features = w_down.shape
        fits = (
            n_col == 4
            and n_row % 4 == 0
            and n_row <= 16
            and tokens.shape[0] % (n_row * PIECE) == 0
            and tokens.shape[0] // (n_row * PIECE) <= 16
            and width % TILE == 0
            and features % TILE == 0
            and tokens.shape[1] * width <= 2 ** 21
            and width * features <= 2 ** 21
        )
        if fits:
            return fused(n_row, tokens, w_gate, w_up, w_down)
        return plain(tokens, w_gate, w_up, w_down)

    in_specs = (P(None, "col"), P("col", "row"), P("col", "row"), P("row", "col"))
    return jax.shard_map(local, mesh=mesh, in_specs=in_specs, out_specs=P("row", "col"), check_vma=False)
```

profile of v0, /device:TPU:0, one launch (start us, length us, event | category | flops | bytes accessed | tf_op | source)
XLA Modules:
  0.0 51.7 jit_solution(11281732780789102620)
XLA Ops:
  0.0 50.1 %shard_map.46 = bf16[64,1024]{1,0:T(8,128)(2,1)} custom-call(bf16[2,2,2,64,1024]{4,3,2,1,0:T(8,128)(2,1)} %bitcast.1, bf16[1024,1280]{1,0:T(8,128)(2,1)} %wg_hbm.1, bf16[1024,1280]{1,0:T(8,128)(2,1)} %wu_hbm.1, bf16[1280,1024]{1,0:T(8,128)(2,1)} %wd_hbm.1), custom_call_target="tpu_custom_call" | custom-call | tf_op jit(solution)/shard_map/pallas_call | solution.py:238
  50.1 1.6 %copy.6 = bf16[64,1024]{1,0:T(8,128)(2,1)} copy(bf16[64,1024]{1,0:T(8,128)(2,1)} %shard_map.46) | data formatting | bytes 262144
where the time goes:
time: 51.8 us; the launch traced here: 51.7 us
  Pallas kernels  50.1 us (97%)
  local copies, waits for them, and re-layouts  1.57 us (3%)
    pallas_call x1, Pallas kernels, fused(): pl.pallas_call(functools.partial(kernel, n_row, sizes), out_shape=jax.Sha...  50.1 us
    unnamed x1, local copies, waits for them, and re-layouts  1.57 us

commit v1 on v0

v1 whole, which is shorter than its diff:
```python
import functools

import jax
import jax.numpy as jnp
from jax import lax
from jax.experimental import pallas as pl
from jax.experimental.pallas import tpu as pltpu
from jax.sharding import PartitionSpec as P

MESH = pl.DeviceIdType.MESH
TILE = 256
SUBS = 2
AHEAD = 3


def activate(pre_gate, pre_up):
    return (jax.nn.gelu(pre_gate, approximate=True) * pre_up).astype(jnp.bfloat16)


def plain(tokens, w_gate, w_up, w_down):
    joined = jnp.concatenate([w_gate, w_up], axis=1)
    hidden_width = w_gate.shape[1]
    summed = lax.psum_scatter(
        jnp.dot(tokens, joined, preferred_element_type=jnp.float32).astype(jnp.bfloat16),
        "col",
        scatter_dimension=0,
        tiled=True,
    ).astype(jnp.float32)
    hidden = activate(summed[:, :hidden_width], summed[:, hidden_width:])
    hidden_all = lax.all_gather(hidden, "col", axis=0, tiled=True)
    result = lax.psum_scatter(
        jnp.dot(hidden_all, w_down, preferred_element_type=jnp.float32),
        "row",
        scatter_dimension=0,
        tiled=True,
    )
    return result.astype(jnp.bfloat16)


def schedule(chunks, ahead):
    late = {"s2": 0, "g1": 2, "s1": -ahead, "g2": 4, "c2": 7, "c1": 6}
    order = []
    for k in range(chunks + max(late.values())):
        for stage, lag in late.items():
            j = k - lag
            if 0 <= j < chunks and (stage != "s1" or j >= ahead):
                order.append((stage, j))
    return order


def kernel(
    n_row, tok_hbm, wg_hbm, wu_hbm, wd_hbm, out_ref,
    tok, w1, wd, s1, own, r1, s2, r2, hid, part, c1s, c1r, c2s, c2r,
    load_sem, send_sem, recv1, recv2, recv3, recv4, recv5, recv6,
):
    row, col = lax.axis_index("row"), lax.axis_index("col")
    y, x = col // 2, col % 2
    z, core = row // 2, row % 2
    n_z = n_row // 2
    chunks = s1.shape[0]
    remote_chunks = chunks - SUBS
    half = hid.shape[-1]
    x_peer = (row, 2 * y + 1 - x)
    y_peer = (row, 2 * (1 - y) + x)
    core_peer = (2 * z + 1 - core, col)
    upper = 2 * z // n_z

    def z_order(k):
        if k == n_z - 1:
            return z
        down = n_z - 1 - k - (z + k + 1) // n_z
        up = k + (k + n_z - z) // n_z
        return down * (1 - upper) + up * upper

    blocks = [z_order(k) for k in range(n_z)]
    z_peers = [(2 * other + core, col) for other in blocks[:-1]]
    first_peer, second_peer = (x_peer, y_peer), (y_peer, x_peer)
    first_at, second_at = (x, y), (y, x)

    barrier = pltpu.get_barrier_semaphore()
    peers = [x_peer, y_peer, core_peer] + z_peers
    for peer in peers:
        pl.semaphore_signal(barrier, inc=1, device_id=peer, device_id_type=MESH)

    def local(src, dst, sem):
        return pltpu.make_async_copy(src, dst, load_sem.at[sem])

    def load_tok(k):
        return local(tok_hbm.at[blocks[k]], tok.at[k], min(k, 1))

    def load_w1(m, k):
        w_hbm = (wg_hbm, wu_hbm)[k]
        return local(w_hbm.at[:, pl.ds(m * half, half)], w1.at[m, :, pl.ds(k * half, half)], 2 + 2 * m + k)

    load_wd = local(wd_hbm, wd, 6)
    load_tok(0).start()
    for k in range(2):
        load_w1(0, k).start()

    def remote(src, dst, send, recv, peer):
        return pltpu.make_async_remote_copy(
            src_ref=src, dst_ref=dst, send_sem=send_sem.at[send], recv_sem=recv, device_id=peer, device_id_type=MESH)

    def copy_s1(m, j):
        return remote(s1.at[j, m], r1.at[j, m], 0, recv1.at[j], first_peer[m])

    def copy_s2(m, j):
        return remote(s2.at[j, m], r2.at[j, m], 1, recv2.at[j], second_peer[m])

    def copy_g1(m, j):
        ref = hid.at[j, m, first_at[m], second_at[m]]
        return remote(ref, ref, 2, recv3.at[j], second_peer[m])

    def copy_g2(m, j):
        ref = hid.at[j, m, first_at[m]]
        return remote(ref, ref, 3, recv4.at[j], first_peer[m])

    def copy_c1(j):
        return remote(c1s.at[j], c1r.at[j], 4, recv5.at[j], core_peer)

    def copy_c2(j):
        k, sub = j // SUBS, j % SUBS
        slot = z - jnp.where(z > blocks[k], 1, 0)
        return remote(c2s.at[j], c2r.at[sub, slot], 5, recv6.at[sub], z_peers[k])

    def arrived(ref, sem):
        remote(ref, ref, 0, sem, x_peer).wait_recv()

    def left(ref, sem):
        remote(ref, ref, sem, recv1.at[0], x_peer).wait_send()

    def rows_of(m, mine, j):
        k, sub = j // SUBS, j % SUBS
        at = first_at[m] if mine else 1 - first_at[m]
        rows = tok[k, :, sub, at] if m == 0 else tok[k, at, sub]
        return rows.reshape(-1, rows.shape[-1])

    def product(m, mine, dst, js, tiles):
        rows = jnp.concatenate([rows_of(m, mine, j) for j in js], axis=0) if len(js) > 1 else rows_of(m, mine, js[0])
        each = rows.shape[0] // len(js)
        for t in tiles:
            columns = slice(t * TILE, (t + 1) * TILE)
            out = jnp.dot(rows, w1[m, :, columns], preferred_element_type=jnp.float32).astype(jnp.bfloat16)
            for i, j in enumerate(js):
                dst[j, m, :, :, columns] = out[i * each:(i + 1) * each].reshape(2, each // 2, TILE)

    def f32(v):
        return v.astype(jnp.float32)

    def do_s1(j):
        for m in range(2):
            copy_s1(m, j).start()

    def do_s2(j):
        arrived(r1.at[j], recv1.at[j])
        for m in range(2):
            at = 1 - second_at[m]
            s2[j, m] = (f32(own[j, m, at]) + f32(r1[j, m, at])).astype(jnp.bfloat16)
            copy_s2(m, j).start()

    def do_g1(j):
        arrived(r2.at[j], recv2.at[j])
        for m in range(2):
            at = second_at[m]
            pre = f32(own[j, m, at]) + f32(r1[j, m, at]) + f32(r2[j, m])
            hid[j, m, first_at[m], at] = activate(pre[:, :half], pre[:, half:])
            copy_g1(m, j).start()

    def do_g2(j):
        arrived(hid.at[j, :, 0, 0], recv3.at[j])
        for m in range(2):
            copy_g2(m, j).start()

    def do_c1(j):
        arrived(hid.at[j, :, 0], recv4.at[j])
        rows = jnp.concatenate([
            jnp.concatenate([hid[j, 0, b, a], hid[j, 1, a, b]], axis=1)
            for a in (1 - core, core) for b in range(2)
        ], axis=0)
        mid = rows.shape[0] // 2
        for t in range(wd.shape[1] // TILE):
            columns = slice(t * TILE, (t + 1) * TILE)
            out = jnp.dot(rows, wd[:, columns], preferred_element_type=jnp.float32)
            c1s[j, :, columns] = out[:mid].astype(jnp.bfloat16)
            part[j, :, columns] = out[mid:]
        copy_c1(j).start()

    def do_c2(j):
        if j < remote_chunks:
            copy_c1(j).wait_recv()
            c2s[j] = (part[j] + f32(c1r[j])).astype(jnp.bfloat16)
            copy_c2(j).start()
        else:
            sub = j % SUBS
            arrived(c2r.at[sub], recv6.at[sub])
            total = part[j]
            for slot in range(n_z - 1):
                total = total + f32(c2r[sub, slot])
            copy_c1(j).wait_recv()
            out_ref[sub] = (total + f32(c1r[j])).astype(jnp.bfloat16)

    stages = {"s1": do_s1, "s2": do_s2, "g1": do_g1, "g2": do_g2, "c1": do_c1, "c2": do_c2}
    ahead = min(AHEAD, chunks)
    tiles = range(w1.shape[2] // TILE)
    early, late = [j for j in range(chunks) if j < 1], [j for j in range(chunks) if j >= 1]

    load_tok(0).wait()
    for k in range(2):
        load_w1(1, k).start()
    for k in range(2):
        load_w1(0, k).wait()
    product(0, False, s1, early, tiles)
    pl.semaphore_wait(barrier, len(peers))
    copy_s1(0, 0).start()
    for k in range(1, n_z):
        load_tok(k).start()
    for k in range(2):
        load_w1(1, k).wait()
    load_wd.start()
    product(1, False, s1, early, tiles)
    copy_s1(1, 0).start()
    local(tok_hbm.at[pl.ds(1, n_z - 1)], tok.at[pl.ds(1, n_z - 1)], 1).wait()
    for m in range(2):
        product(m, False, s1, late, tiles)
        for j in range(1, ahead):
            copy_s1(m, j).start()
    for m in range(2):
        product(m, True, own, range(chunks), tiles)
    load_wd.wait()

    for stage, j in schedule(chunks, ahead):
        stages[stage](j)

    for ref, sem in ((s1, 0), (s2, 1), (hid.at[:, :, 0, 0], 2), (hid.at[:, :, 0], 3), (c1s, 4), (c2s, 5)):
        left(ref, sem)


def fused(n_row, tokens, w_gate, w_up, w_down):
    n_tok, depth = tokens.shape
    width, features = w_down.shape
    per_row = n_tok // n_row
    n_z, half = n_row // 2, width // 2
    each = per_row // (2 * SUBS)
    chunks = n_z * SUBS
    bf16, dma = jnp.bfloat16, pltpu.SemaphoreType.DMA
    out = pl.pallas_call(
        functools.partial(kernel, n_row),
        out_shape=pltpu.VMEM((SUBS, 2 * each, features), bf16),
        in_specs=[pl.BlockSpec(memory_space=pl.ANY)] * 4,
        out_specs=pl.BlockSpec(memory_space=pltpu.VMEM),
        scratch_shapes=[
            pltpu.VMEM((n_z, 2, SUBS, 2, each, depth), bf16),
            pltpu.VMEM((2, depth, width), bf16),
            pltpu.VMEM((width, features), bf16),
            pltpu.VMEM((chunks, 2, 2, each, width), bf16),
            pltpu.VMEM((chunks, 2, 2, each, width), bf16),
            pltpu.VMEM((chunks, 2, 2, each, width), bf16),
            pltpu.VMEM((chunks, 2, each, width), bf16),
            pltpu.VMEM((chunks, 2, each, width), bf16),
            pltpu.VMEM((chunks, 2, 2, 2, each, half), bf16),
            pltpu.VMEM((chunks, 2 * each, features), jnp.float32),
            pltpu.VMEM((chunks, 2 * each, features), bf16),
            pltpu.VMEM((chunks, 2 * each, features), bf16),
            pltpu.VMEM((chunks - SUBS, 2 * each, features), bf16),
            pltpu.VMEM((SUBS, n_z - 1, 2 * each, features), bf16),
            dma((7,)), dma((6,)),
            dma((chunks,)), dma((chunks,)), dma((chunks,)), dma((chunks,)), dma((chunks,)), dma((SUBS,)),
        ],
        compiler_params=pltpu.CompilerParams(
            collective_id=0, has_side_effects=True, vmem_limit_bytes=62914560
        ),
    )(tokens.reshape(n_z, 2, SUBS, 2, each, depth), w_gate, w_up, w_down)
    return out.reshape(per_row, features)


def solution(mesh):
    n_row, n_col = mesh.shape["row"], mesh.shape["col"]

    def local(tokens, w_gate, w_up, w_down):
        width, features = w_down.shape
        fits = (
            n_col == 4
            and 4 <= n_row <= 16
            and n_row % 2 == 0
            and tokens.shape[0] % (n_row * 32 * SUBS) == 0
            and tokens.shape[0] <= 1024
            and width % TILE == 0
            and features % TILE == 0
            and tokens.shape[1] * width <= 2 ** 21
            and width * features <= 2 ** 21
        )
        if fits:
            return fused(n_row, tokens, w_gate, w_up, w_down)
        return plain(tokens, w_gate, w_up, w_down)

    in_specs = (P(None, "col"), P("col", "row"), P("col", "row"), P("row", "col"))
    return jax.shard_map(local, mesh=mesh, in_specs=in_specs, out_specs=P("row", "col"), check_vma=False)
```

time: 51.8 us -> 45.5 us (0.88)
  Pallas kernels: 50.1 us -> 44.7 us
  local copies, waits for them, and re-layouts: 1.57 us -> 0.66 us
    pallas_call x1, Pallas kernels: 50.1 us -> 44.7 us  [fused(): pl.pallas_call(functools.partial(kernel, n_row), out_shape=pltpu.VMEM((SU...]
    unnamed x1, local copies, waits for them, and re-layouts: 1.57 us -> 0.66 us
where the time goes in v1:
time: 45.5 us; the launch traced here: 45.3 us
  Pallas kernels  44.7 us (98%)
  local copies, waits for them, and re-layouts  0.66 us (1%)
    pallas_call x1, Pallas kernels, fused(): pl.pallas_call(functools.partial(kernel, n_row), out_shape=pltpu.VMEM((SU...  44.7 us

profile of v1, /device:TPU:0, one launch (start us, length us, event | category | flops | bytes accessed | tf_op | source)
XLA Modules:
  0.0 45.3 jit_solution(13664536662328782893)
XLA Ops:
  0.0 44.7 %shard_map.46 = bf16[2,32,1024]{2,1,0:T(8,128)(2,1)S(1)} custom-call(bf16[4,2,2,2,16,1024]{5,4,3,2,1,0:T(8,128)(2,1)} %bitcast.3, bf16[1024,1280]{1,0:T(8,128)(2,1)} %wg_hbm.1, bf16[1024,1280]{1,0:T(8,128)(2,1)} %wu_hbm.1, bf16[1280,1024]{1,0:T(8,128)(2,1)} %wd_hbm.1), custom_call_target="tpu_custom_call" | custom-call | tf_op jit(solution)/shard_map/pallas_call | solution.py:246
  44.7 0.7 %copy.6 = bf16[64,1024]{1,0:T(8,128)(2,1)} copy(bf16[64,1024]{1,0:T(8,128)(2,1)S(1)} %bitcast.2) | data formatting | bytes 262144

commit v2 on v1

--- a/solution.py
+++ b/solution.py
@@ -11,6 +11,7 @@
 TILE = 256
 SUBS = 2
 AHEAD = 3
+FLIGHT = 6
 
 
 def activate(pre_gate, pre_up):
@@ -51,7 +52,7 @@
 def kernel(
     n_row, tok_hbm, wg_hbm, wu_hbm, wd_hbm, out_ref,
     tok, w1, wd, s1, own, r1, s2, r2, hid, part, c1s, c1r, c2s, c2r,
-    load_sem, send_sem, recv1, recv2, recv3, recv4, recv5, recv6,
+    load_sem, send_sem, recv1, recv2, recv3, recv4, recv5, recv6, ready,
 ):
     row, col = lax.axis_index("row"), lax.axis_index("col")
     y, x = col // 2, col % 2
@@ -63,39 +64,69 @@
     x_peer = (row, 2 * y + 1 - x)
     y_peer = (row, 2 * (1 - y) + x)
     core_peer = (2 * z + 1 - core, col)
-    upper = 2 * z // n_z
 
     def z_order(k):
-        if k == n_z - 1:
-            return z
-        down = n_z - 1 - k - (z + k + 1) // n_z
-        up = k + (k + n_z - z) // n_z
-        return down * (1 - upper) + up * upper
+        return z if k == n_z - 1 else jnp.where(z > k, k, n_z - 1 - k + z)
 
     blocks = [z_order(k) for k in range(n_z)]
+    below, above = z > 0, z < n_z - 1
     z_peers = [(2 * other + core, col) for other in blocks[:-1]]
     first_peer, second_peer = (x_peer, y_peer), (y_peer, x_peer)
     first_at, second_at = (x, y), (y, x)
 
     barrier = pltpu.get_barrier_semaphore()
-    peers = [x_peer, y_peer, core_peer] + z_peers
-    for peer in peers:
+    for peer in (x_peer, y_peer, core_peer):
         pl.semaphore_signal(barrier, inc=1, device_id=peer, device_id_type=MESH)
+    z_above, z_below = (row + 2, col), (row - 2, col)
+    for there, peer in ((above, z_above), (below, z_below)):
+        @pl.when(there)
+        def _():
+            pl.semaphore_signal(barrier, inc=1, device_id=peer, device_id_type=MESH)
+
+    def enter():
+        pl.semaphore_wait(barrier, 3 + jnp.where(above, 1, 0) + jnp.where(below, 1, 0))
+
+    def relay(d):
+        for side, (here, there, peer) in enumerate(
+            ((z >= d, above, z_above), (z <= n_z - 1 - d, below, z_below))
+        ):
+            @pl.when(jnp.logical_and(here, there))
+            def _():
+                pl.semaphore_signal(ready.at[d - 1, side], inc=1, device_id=peer, device_id_type=MESH)
+
+    def relayed(d):
+        for side, here in enumerate((z > d, z < n_z - 1 - d)):
+            @pl.when(here)
+            def _():
+                pl.semaphore_wait(ready.at[d - 1, side], 1)
 
     def local(src, dst, sem):
         return pltpu.make_async_copy(src, dst, load_sem.at[sem])
 
+    n_tiles = w1.shape[2] // TILE
+
     def load_tok(k):
         return local(tok_hbm.at[blocks[k]], tok.at[k], min(k, 1))
 
-    def load_w1(m, k):
-        w_hbm = (wg_hbm, wu_hbm)[k]
-        return local(w_hbm.at[:, pl.ds(m * half, half)], w1.at[m, :, pl.ds(k * half, half)], 2 + 2 * m + k)
-
-    load_wd = local(wd_hbm, wd, 6)
+    def load_w1(m, t):
+        for k, w_hbm in enumerate((wg_hbm, wu_hbm)):
+            low, high = max(t * TILE, k * half), min((t + 1) * TILE, (k + 1) * half)
+            if low < high:
+                local(
+                    w_hbm.at[:, pl.ds(m * half + low - k * half, high - low)],
+                    w1.at[m, :, pl.ds(low, high - low)],
+                    3 + 2 * t + m,
+                ).start()
+
+    def wait_w1(m, t):
+        columns = pl.ds(t * TILE, TILE)
+        local(wg_hbm.at[:, pl.ds(0, TILE)], w1.at[m, :, columns], 3 + 2 * t + m).wait()
+
+    load_wd = local(wd_hbm, wd, 2)
+    order_w1 = [(m, t) for t in range(n_tiles) for m in range(2)]
     load_tok(0).start()
-    for k in range(2):
-        load_w1(0, k).start()
+    for m, t in order_w1[:FLIGHT]:
+        load_w1(m, t)
 
     def remote(src, dst, send, recv, peer):
         return pltpu.make_async_remote_copy(
@@ -201,31 +232,40 @@
 
     stages = {"s1": do_s1, "s2": do_s2, "g1": do_g1, "g2": do_g2, "c1": do_c1, "c2": do_c2}
     ahead = min(AHEAD, chunks)
-    tiles = range(w1.shape[2] // TILE)
-    early, late = [j for j in range(chunks) if j < 1], [j for j in range(chunks) if j >= 1]
+    tiles = range(n_tiles)
+    early, late = range(SUBS), range(SUBS, chunks)
+
+    def copy_tile(m, t):
+        columns = pl.ds(t * TILE, TILE)
+        return remote(s1.at[0, m, :, :, columns], r1.at[0, m, :, :, columns], 0, recv1.at[0], first_peer[m])
 
     load_tok(0).wait()
-    for k in range(2):
-        load_w1(1, k).start()
-    for k in range(2):
-        load_w1(0, k).wait()
-    product(0, False, s1, early, tiles)
-    pl.semaphore_wait(barrier, len(peers))
-    copy_s1(0, 0).start()
-    for k in range(1, n_z):
-        load_tok(k).start()
-    for k in range(2):
-        load_w1(1, k).wait()
+    for i, (m, t) in enumerate(order_w1):
+        wait_w1(m, t)
+        if i + FLIGHT < len(order_w1):
+            load_w1(*order_w1[i + FLIGHT])
+        elif i + FLIGHT == len(order_w1):
+            for k in range(1, n_z):
+                load_tok(k).start()
+        product(m, False, s1, early, [t])
+        if i == 0:
+            enter()
+            relay(1)
+        copy_tile(m, t).start()
     load_wd.start()
-    product(1, False, s1, early, tiles)
-    copy_s1(1, 0).start()
+    for j in range(1, min(ahead, SUBS)):
+        do_s1(j)
     local(tok_hbm.at[pl.ds(1, n_z - 1)], tok.at[pl.ds(1, n_z - 1)], 1).wait()
     for m in range(2):
         product(m, False, s1, late, tiles)
-        for j in range(1, ahead):
+        for j in range(SUBS, ahead):
             copy_s1(m, j).start()
     for m in range(2):
         product(m, True, own, range(chunks), tiles)
+    for d in range(1, n_z - 1):
+        relayed(d)
+        if d < n_z - 2:
+            relay(d + 1)
     load_wd.wait()
 
     for stage, j in schedule(chunks, ahead):
@@ -263,8 +303,9 @@
             pltpu.VMEM((chunks, 2 * each, features), bf16),
             pltpu.VMEM((chunks - SUBS, 2 * each, features), bf16),
             pltpu.VMEM((SUBS, n_z - 1, 2 * each, features), bf16),
-            dma((7,)), dma((6,)),
+            dma((3 + 2 * (width // TILE),)), dma((6,)),
             dma((chunks,)), dma((chunks,)), dma((chunks,)), dma((chunks,)), dma((chunks,)), dma((SUBS,)),
+            pltpu.SemaphoreType.REGULAR((n_z - 2, 2)),
         ],
         compiler_params=pltpu.CompilerParams(
             collective_id=0, has_side_effects=True, vmem_limit_bytes=62914560
@@ -280,7 +321,7 @@
         width, features = w_down.shape
         fits = (
             n_col == 4
-            and 4 <= n_row <= 16
+            and 6 <= n_row <= 16
             and n_row % 2 == 0
             and tokens.shape[0] % (n_row * 32 * SUBS) == 0
             and tokens.shape[0] <= 1024

time: 45.5 us -> 44.6 us (0.980)
  the two profiles are of different devices: /device:TPU:0 before, /device:TPU:17 now
where the time goes in v2:
time: 44.6 us; the launch traced here: 44.4 us
  Pallas kernels  43.8 us (98%)
  local copies, waits for them, and re-layouts  0.66 us (1%)
    pallas_call x1, Pallas kernels, fused(): pl.pallas_call(functools.partial(kernel, n_row), out_shape=pltpu.VMEM((SU...  43.8 us

profile of v2, /device:TPU:17, one launch (start us, length us, event | category | flops | bytes accessed | tf_op | source)
XLA Modules:
  0.0 44.4 jit_solution(13915815713068932236)
XLA Ops:
  0.0 43.8 %shard_map.46 = bf16[2,32,1024]{2,1,0:T(8,128)(2,1)S(1)} custom-call(bf16[4,2,2,2,16,1024]{5,4,3,2,1,0:T(8,128)(2,1)} %bitcast.3, bf16[1024,1280]{1,0:T(8,128)(2,1)} %wg_hbm.1, bf16[1024,1280]{1,0:T(8,128)(2,1)} %wu_hbm.1, bf16[1280,1024]{1,0:T(8,128)(2,1)} %wd_hbm.1), custom_call_target="tpu_custom_call" | custom-call | tf_op jit(solution)/shard_map/pallas_call | solution.py:286
  43.8 0.7 %copy.6 = bf16[64,1024]{1,0:T(8,128)(2,1)} copy(bf16[64,1024]{1,0:T(8,128)(2,1)S(1)} %bitcast.2) | data formatting | bytes 262144

commit v3 on v2

--- a/solution.py
+++ b/solution.py
@@ -10,7 +10,9 @@
 MESH = pl.DeviceIdType.MESH
 TILE = 256
 SUBS = 2
-AHEAD = 3
+MERGED = (6,)
+DIRECT = (6, 7)
+AHEAD = 4
 FLIGHT = 6
 
 
@@ -38,21 +40,24 @@
     return result.astype(jnp.bfloat16)
 
 
+ORDER = (
+    ("s2", 1), ("s2", 0), ("s1", 5), ("s2", 2), ("s2", 3), ("g1", 1), ("g1", 0), ("s1", 4),
+    ("s2", 5), ("g1", 2), ("g2", 1), ("g1", 3), ("g2", 0), ("s1", 6), ("g1", 5), ("g2", 2),
+    ("c1", 1), ("c2", 1), ("s2", 4), ("g2", 3), ("s1", 7), ("c1", 0), ("s2", 6), ("c2", 0),
+    ("c1", 2), ("g1", 4), ("c1", 3), ("g2", 5), ("c2", 2), ("s2", 7), ("g2", 4), ("g1", 6),
+    ("c2", 3), ("c1", 5), ("g1", 7), ("c2", 5), ("c1", 4), ("c2", 4), ("c1", 6), ("c2", 7),
+    ("c2", 6),
+)
+
+
 def schedule(chunks, ahead):
-    late = {"s2": 0, "g1": 2, "s1": -ahead, "g2": 4, "c2": 7, "c1": 6}
-    order = []
-    for k in range(chunks + max(late.values())):
-        for stage, lag in late.items():
-            j = k - lag
-            if 0 <= j < chunks and (stage != "s1" or j >= ahead):
-                order.append((stage, j))
-    return order
+    return ORDER
 
 
 def kernel(
     n_row, tok_hbm, wg_hbm, wu_hbm, wd_hbm, out_ref,
     tok, w1, wd, s1, own, r1, s2, r2, hid, part, c1s, c1r, c2s, c2r,
-    load_sem, send_sem, recv1, recv2, recv3, recv4, recv5, recv6, ready,
+    load_sem, send_sem, recv1, recv2, recv3, recv5, recv6, ready,
 ):
     row, col = lax.axis_index("row"), lax.axis_index("col")
     y, x = col // 2, col % 2
@@ -64,9 +69,15 @@
     x_peer = (row, 2 * y + 1 - x)
     y_peer = (row, 2 * (1 - y) + x)
     core_peer = (2 * z + 1 - core, col)
+    diagonal = (row, 3 - col)
 
     def z_order(k):
-        return z if k == n_z - 1 else jnp.where(z > k, k, n_z - 1 - k + z)
+        if k == n_z - 1:
+            return z
+        order = jnp.where(z > k, k, n_z - 1 - k + z)
+        if n_z == 4:
+            order = jnp.where(z == 1, (3, 0, 2)[k], order)
+        return order
 
     blocks = [z_order(k) for k in range(n_z)]
     below, above = z > 0, z < n_z - 1
@@ -75,7 +86,8 @@
     first_at, second_at = (x, y), (y, x)
 
     barrier = pltpu.get_barrier_semaphore()
-    for peer in (x_peer, y_peer, core_peer):
+    near = (x_peer, y_peer, core_peer) + ((diagonal,) if DIRECT else ())
+    for peer in near:
         pl.semaphore_signal(barrier, inc=1, device_id=peer, device_id_type=MESH)
     z_above, z_below = (row + 2, col), (row - 2, col)
     for there, peer in ((above, z_above), (below, z_below)):
@@ -84,7 +96,7 @@
             pl.semaphore_signal(barrier, inc=1, device_id=peer, device_id_type=MESH)
 
     def enter():
-        pl.semaphore_wait(barrier, 3 + jnp.where(above, 1, 0) + jnp.where(below, 1, 0))
+        pl.semaphore_wait(barrier, len(near) + jnp.where(above, 1, 0) + jnp.where(below, 1, 0))
 
     def relay(d):
         for side, (here, there, peer) in enumerate(
@@ -115,12 +127,12 @@
                 local(
                     w_hbm.at[:, pl.ds(m * half + low - k * half, high - low)],
                     w1.at[m, :, pl.ds(low, high - low)],
-                    3 + 2 * t + m,
+                    3 + (2 * t + m) % FLIGHT,
                 ).start()
 
     def wait_w1(m, t):
         columns = pl.ds(t * TILE, TILE)
-        local(wg_hbm.at[:, pl.ds(0, TILE)], w1.at[m, :, columns], 3 + 2 * t + m).wait()
+        local(wg_hbm.at[:, pl.ds(0, TILE)], w1.at[m, :, columns], 3 + (2 * t + m) % FLIGHT).wait()
 
     load_wd = local(wd_hbm, wd, 2)
     order_w1 = [(m, t) for t in range(n_tiles) for m in range(2)]
@@ -140,11 +152,15 @@
 
     def copy_g1(m, j):
         ref = hid.at[j, m, first_at[m], second_at[m]]
-        return remote(ref, ref, 2, recv3.at[j], second_peer[m])
+        return remote(ref, ref, 2, recv1.at[j], second_peer[m])
 
     def copy_g2(m, j):
         ref = hid.at[j, m, first_at[m]]
-        return remote(ref, ref, 3, recv4.at[j], first_peer[m])
+        return remote(ref, ref, 3, recv2.at[j], first_peer[m])
+
+    def copy_gd(m, j, peer):
+        ref = hid.at[j, m, first_at[m], second_at[m]]
+        return remote(ref, ref, 6, recv3.at[j - remote_chunks], peer)
 
     def copy_c1(j):
         return remote(c1s.at[j], c1r.at[j], 4, recv5.at[j], core_peer)
@@ -195,26 +211,40 @@
             at = second_at[m]
             pre = f32(own[j, m, at]) + f32(r1[j, m, at]) + f32(r2[j, m])
             hid[j, m, first_at[m], at] = activate(pre[:, :half], pre[:, half:])
-            copy_g1(m, j).start()
+            if j in DIRECT:
+                copy_gd(m, j, x_peer).start()
+                copy_gd(m, j, y_peer).start()
+            else:
+                copy_g1(m, j).start()
+        if j in DIRECT:
+            for m in range(2):
+                copy_gd(m, j, diagonal).start()
 
     def do_g2(j):
-        arrived(hid.at[j, :, 0, 0], recv3.at[j])
+        arrived(hid.at[j, :, 0, 0], recv1.at[j])
         for m in range(2):
             copy_g2(m, j).start()
 
     def do_c1(j):
-        arrived(hid.at[j, :, 0], recv4.at[j])
+        js = (j, j + 1) if j in MERGED else (j,)
+        for i in js:
+            if i in DIRECT:
+                arrived(hid.at[:3, :, 0, 0], recv3.at[i - remote_chunks])
+            else:
+                arrived(hid.at[i, :, 0], recv2.at[i])
         rows = jnp.concatenate([
-            jnp.concatenate([hid[j, 0, b, a], hid[j, 1, a, b]], axis=1)
-            for a in (1 - core, core) for b in range(2)
+            jnp.concatenate([hid[i, 0, b, a], hid[i, 1, a, b]], axis=1)
+            for a in (1 - core, core) for i in js for b in range(2)
         ], axis=0)
-        mid = rows.shape[0] // 2
+        mid, each = rows.shape[0] // 2, rows.shape[0] // 2 // len(js)
         for t in range(wd.shape[1] // TILE):
             columns = slice(t * TILE, (t + 1) * TILE)
             out = jnp.dot(rows, wd[:, columns], preferred_element_type=jnp.float32)
-            c1s[j, :, columns] = out[:mid].astype(jnp.bfloat16)
-            part[j, :, columns] = out[mid:]
-        copy_c1(j).start()
+            for n, i in enumerate(js):
+                c1s[i, :, columns] = out[n * each:(n + 1) * each].astype(jnp.bfloat16)
+                part[i, :, columns] = out[mid + n * each:mid + (n + 1) * each]
+        for i in js:
+            copy_c1(i).start()
 
     def do_c2(j):
         if j < remote_chunks:
@@ -235,9 +265,9 @@
     tiles = range(n_tiles)
     early, late = range(SUBS), range(SUBS, chunks)
 
-    def copy_tile(m, t):
+    def copy_tile(m, t, j):
         columns = pl.ds(t * TILE, TILE)
-        return remote(s1.at[0, m, :, :, columns], r1.at[0, m, :, :, columns], 0, recv1.at[0], first_peer[m])
+        return remote(s1.at[j, m, :, :, columns], r1.at[j, m, :, :, columns], 0, recv1.at[j], first_peer[m])
 
     load_tok(0).wait()
     for i, (m, t) in enumerate(order_w1):
@@ -251,10 +281,9 @@
         if i == 0:
             enter()
             relay(1)
-        copy_tile(m, t).start()
+        for j in early:
+            copy_tile(m, t, j).start()
     load_wd.start()
-    for j in range(1, min(ahead, SUBS)):
-        do_s1(j)
     local(tok_hbm.at[pl.ds(1, n_z - 1)], tok.at[pl.ds(1, n_z - 1)], 1).wait()
     for m in range(2):
         product(m, False, s1, late, tiles)
@@ -271,7 +300,11 @@
     for stage, j in schedule(chunks, ahead):
         stages[stage](j)
 
-    for ref, sem in ((s1, 0), (s2, 1), (hid.at[:, :, 0, 0], 2), (hid.at[:, :, 0], 3), (c1s, 4), (c2s, 5)):
+    paired = chunks - len(DIRECT)
+    waits = [(s1, 0), (s2, 1), (hid.at[:paired, :, 0, 0], 2), (hid.at[:paired, :, 0], 3), (c1s, 4), (c2s, 5)]
+    if DIRECT:
+        waits.append((hid.at[:3 * len(DIRECT), :, 0, 0], 6))
+    for ref, sem in waits:
         left(ref, sem)
 
 
@@ -303,8 +336,8 @@
             pltpu.VMEM((chunks, 2 * each, features), bf16),
             pltpu.VMEM((chunks - SUBS, 2 * each, features), bf16),
             pltpu.VMEM((SUBS, n_z - 1, 2 * each, features), bf16),
-            dma((3 + 2 * (width // TILE),)), dma((6,)),
-            dma((chunks,)), dma((chunks,)), dma((chunks,)), dma((chunks,)), dma((chunks,)), dma((SUBS,)),
+            dma((3 + FLIGHT,)), dma((7,)),
+            dma((chunks,)), dma((chunks,)), dma((SUBS,)), dma((chunks,)), dma((SUBS,)),
             pltpu.SemaphoreType.REGULAR((n_z - 2, 2)),
         ],
         compiler_params=pltpu.CompilerParams(

time: 44.6 us -> 41.8 us (0.937)
  the two profiles are of different devices: /device:TPU:17 before, /device:TPU:0 now
where the time goes in v3:
time: 41.8 us; the launch traced here: 41.6 us
  Pallas kernels  40.9 us (98%)
  local copies, waits for them, and re-layouts  0.66 us (2%)
    pallas_call x1, Pallas kernels, fused(): pl.pallas_call(functools.partial(kernel, n_row), out_shape=pltpu.VMEM((SU...  40.9 us

profile of v3, /device:TPU:0, one launch (start us, length us, event | category | flops | bytes accessed | tf_op | source)
XLA Modules:
  0.0 41.6 jit_solution(15828322578248026152)
XLA Ops:
  0.0 40.9 %shard_map.46 = bf16[2,32,1024]{2,1,0:T(8,128)(2,1)S(1)} custom-call(bf16[4,2,2,2,16,1024]{5,4,3,2,1,0:T(8,128)(2,1)} %bitcast.3, bf16[1024,1280]{1,0:T(8,128)(2,1)} %wg_hbm.1, bf16[1024,1280]{1,0:T(8,128)(2,1)} %wu_hbm.1, bf16[1280,1024]{1,0:T(8,128)(2,1)} %wd_hbm.1), custom_call_target="tpu_custom_call" | custom-call | tf_op jit(solution)/shard_map/pallas_call | solution.py:319
  41.0 0.7 %copy.6 = bf16[64,1024]{1,0:T(8,128)(2,1)} copy(bf16[64,1024]{1,0:T(8,128)(2,1)S(1)} %bitcast.2) | data formatting | bytes 262144

commit v4 on v3

--- a/solution.py
+++ b/solution.py
@@ -12,8 +12,8 @@
 SUBS = 2
 MERGED = (6,)
 DIRECT = (6, 7)
-AHEAD = 4
-FLIGHT = 6
+AHEAD = 3
+FLIGHT = 8
 
 
 def activate(pre_gate, pre_up):
@@ -41,23 +41,23 @@
 
 
 ORDER = (
-    ("s2", 1), ("s2", 0), ("s1", 5), ("s2", 2), ("s2", 3), ("g1", 1), ("g1", 0), ("s1", 4),
-    ("s2", 5), ("g1", 2), ("g2", 1), ("g1", 3), ("g2", 0), ("s1", 6), ("g1", 5), ("g2", 2),
-    ("c1", 1), ("c2", 1), ("s2", 4), ("g2", 3), ("s1", 7), ("c1", 0), ("s2", 6), ("c2", 0),
-    ("c1", 2), ("g1", 4), ("c1", 3), ("g2", 5), ("c2", 2), ("s2", 7), ("g2", 4), ("g1", 6),
-    ("c2", 3), ("c1", 5), ("g1", 7), ("c2", 5), ("c1", 4), ("c2", 4), ("c1", 6), ("c2", 7),
-    ("c2", 6),
+    ("s1", 3), ("s2", 1), ("s1", 5), ("s2", 2), ("s2", 0), ("s2", 3), ("g1", 1), ("s1", 4),
+    ("g1", 2), ("s2", 5), ("g2", 1), ("g1", 0), ("g2", 2), ("g1", 3), ("s2", 4), ("g1", 5),
+    ("s1", 6), ("c1", 1), ("c2", 1), ("g2", 0), ("s1", 7), ("g2", 3), ("c1", 2), ("g1", 4),
+    ("c2", 2), ("s2", 6), ("g2", 5), ("c1", 0), ("c2", 0), ("s2", 7), ("c1", 3), ("g2", 4),
+    ("g1", 6), ("c2", 3), ("c1", 5), ("g1", 7), ("c2", 5), ("c1", 4), ("c2", 4), ("c1", 6),
+    ("c2", 7), ("c2", 6),
 )
 
 
 def schedule(chunks, ahead):
-    return ORDER
+    return ORDER, ORDER
 
 
 def kernel(
     n_row, tok_hbm, wg_hbm, wu_hbm, wd_hbm, out_ref,
-    tok, w1, wd, s1, own, r1, s2, r2, hid, part, c1s, c1r, c2s, c2r,
-    load_sem, send_sem, recv1, recv2, recv3, recv5, recv6, ready,
+    tok, w1, wd, s1, own, r1, s2, r2, hid, part, acc, c1s, c1r, c2s, c2r,
+    load_sem, send_sem, recv1, recv2, recv3, recv5, recv6, ready, ready_diagonal,
 ):
     row, col = lax.axis_index("row"), lax.axis_index("col")
     y, x = col // 2, col % 2
@@ -69,7 +69,6 @@
     x_peer = (row, 2 * y + 1 - x)
     y_peer = (row, 2 * (1 - y) + x)
     core_peer = (2 * z + 1 - core, col)
-    diagonal = (row, 3 - col)
 
     def z_order(k):
         if k == n_z - 1:
@@ -86,7 +85,7 @@
     first_at, second_at = (x, y), (y, x)
 
     barrier = pltpu.get_barrier_semaphore()
-    near = (x_peer, y_peer, core_peer) + ((diagonal,) if DIRECT else ())
+    near = (x_peer, y_peer, core_peer)
     for peer in near:
         pl.semaphore_signal(barrier, inc=1, device_id=peer, device_id_type=MESH)
     z_above, z_below = (row + 2, col), (row - 2, col)
@@ -160,7 +159,7 @@
 
     def copy_gd(m, j, peer):
         ref = hid.at[j, m, first_at[m], second_at[m]]
-        return remote(ref, ref, 6, recv3.at[j - remote_chunks], peer)
+        return remote(ref, ref, 6, recv3.at[2 * (j - remote_chunks) + m], peer)
 
     def copy_c1(j):
         return remote(c1s.at[j], c1r.at[j], 4, recv5.at[j], core_peer)
@@ -211,40 +210,56 @@
             at = second_at[m]
             pre = f32(own[j, m, at]) + f32(r1[j, m, at]) + f32(r2[j, m])
             hid[j, m, first_at[m], at] = activate(pre[:, :half], pre[:, half:])
-            if j in DIRECT:
-                copy_gd(m, j, x_peer).start()
-                copy_gd(m, j, y_peer).start()
-            else:
+            if j not in DIRECT:
                 copy_g1(m, j).start()
         if j in DIRECT:
-            for m in range(2):
-                copy_gd(m, j, diagonal).start()
+            for k in range(3):
+                for m in range(2):
+                    copy_gd(m, j, (row, k + jnp.where(k >= col, 1, 0))).start()
 
     def do_g2(j):
         arrived(hid.at[j, :, 0, 0], recv1.at[j])
         for m in range(2):
             copy_g2(m, j).start()
 
+    def hidden_rows(m, js):
+        return jnp.concatenate([
+            hid[j, 0, b, a] if m == 0 else hid[j, 1, a, b]
+            for a in (1 - core, core) for j in js for b in range(2)
+        ], axis=0)
+
     def do_c1(j):
-        js = (j, j + 1) if j in MERGED else (j,)
-        for i in js:
-            if i in DIRECT:
-                arrived(hid.at[:3, :, 0, 0], recv3.at[i - remote_chunks])
-            else:
-                arrived(hid.at[i, :, 0], recv2.at[i])
-        rows = jnp.concatenate([
-            jnp.concatenate([hid[i, 0, b, a], hid[i, 1, a, b]], axis=1)
-            for a in (1 - core, core) for i in js for b in range(2)
-        ], axis=0)
-        mid, each = rows.shape[0] // 2, rows.shape[0] // 2 // len(js)
+        if j in DIRECT:
+            do_own(range(j, chunks))
+            return
+        arrived(hid.at[j, :, 0], recv2.at[j])
+        rows = jnp.concatenate([hidden_rows(m, [j]) for m in range(2)], axis=1)
+        mid = rows.shape[0] // 2
         for t in range(wd.shape[1] // TILE):
             columns = slice(t * TILE, (t + 1) * TILE)
             out = jnp.dot(rows, wd[:, columns], preferred_element_type=jnp.float32)
-            for n, i in enumerate(js):
-                c1s[i, :, columns] = out[n * each:(n + 1) * each].astype(jnp.bfloat16)
-                part[i, :, columns] = out[mid + n * each:mid + (n + 1) * each]
-        for i in js:
-            copy_c1(i).start()
+            c1s[j, :, columns] = out[:mid].astype(jnp.bfloat16)
+            part[j, :, columns] = out[mid:]
+        copy_c1(j).start()
+
+    def do_own(js):
+        for m in range(2):
+            for j in js:
+                arrived(hid.at[:3, 0, 0, 0], recv3.at[2 * (j - remote_chunks) + m])
+            rows = hidden_rows(m, js)
+            mid, each = rows.shape[0] // 2, rows.shape[0] // 2 // len(js)
+            for t in range(wd.shape[1] // TILE):
+                columns = slice(t * TILE, (t + 1) * TILE)
+                out = jnp.dot(rows, wd[m * half:(m + 1) * half, columns], preferred_element_type=jnp.float32)
+                if m == 0:
+                    acc[:, columns] = out
+                    continue
+                out = out + acc[:, columns]
+                for n, j in enumerate(js):
+                    c1s[j, :, columns] = out[n * each:(n + 1) * each].astype(jnp.bfloat16)
+                    part[j, :, columns] = out[mid + n * each:mid + (n + 1) * each]
+        for j in js:
+            copy_c1(j).start()
 
     def do_c2(j):
         if j < remote_chunks:
@@ -281,6 +296,7 @@
         if i == 0:
             enter()
             relay(1)
+            pl.semaphore_signal(ready_diagonal, inc=1, device_id=x_peer, device_id_type=MESH)
         for j in early:
             copy_tile(m, t, j).start()
     load_wd.start()
@@ -291,15 +307,30 @@
             copy_s1(m, j).start()
     for m in range(2):
         product(m, True, own, range(chunks), tiles)
-    for d in range(1, n_z - 1):
+    for d in range(1, n_z - 2):
         relayed(d)
-        if d < n_z - 2:
-            relay(d + 1)
-    load_wd.wait()
-
-    for stage, j in schedule(chunks, ahead):
-        stages[stage](j)
-
+        relay(d + 1)
+    def run(order):
+        known = set()
+        for stage, j in order:
+            if stage == "c1" and stage not in known:
+                load_wd.wait()
+                relayed(n_z - 2)
+            if stage == "g1" and j in DIRECT and "diagonal" not in known:
+                known.add("diagonal")
+                pl.semaphore_wait(ready_diagonal, 1)
+            known.add(stage)
+            stages[stage](j)
+
+    orders = schedule(chunks, ahead)
+    if orders[0] == orders[1]:
+        run(orders[0])
+    else:
+        for c in range(2):
+            pl.when(core == c)(functools.partial(run, orders[c]))
+
+    if not DIRECT:
+        pl.semaphore_wait(ready_diagonal, 1)
     paired = chunks - len(DIRECT)
     waits = [(s1, 0), (s2, 1), (hid.at[:paired, :, 0, 0], 2), (hid.at[:paired, :, 0], 3), (c1s, 4), (c2s, 5)]
     if DIRECT:
@@ -332,13 +363,15 @@
             pltpu.VMEM((chunks, 2, each, width), bf16),
             pltpu.VMEM((chunks, 2, 2, 2, each, half), bf16),
             pltpu.VMEM((chunks, 2 * each, features), jnp.float32),
+            pltpu.VMEM((4 * SUBS * each, features), jnp.float32),
             pltpu.VMEM((chunks, 2 * each, features), bf16),
             pltpu.VMEM((chunks, 2 * each, features), bf16),
             pltpu.VMEM((chunks - SUBS, 2 * each, features), bf16),
             pltpu.VMEM((SUBS, n_z - 1, 2 * each, features), bf16),
             dma((3 + FLIGHT,)), dma((7,)),
-            dma((chunks,)), dma((chunks,)), dma((SUBS,)), dma((chunks,)), dma((SUBS,)),
+            dma((chunks,)), dma((chunks,)), dma((2 * SUBS,)), dma((chunks,)), dma((SUBS,)),
             pltpu.SemaphoreType.REGULAR((n_z - 2, 2)),
+            pltpu.SemaphoreType.REGULAR,
         ],
         compiler_params=pltpu.CompilerParams(
             collective_id=0, has_side_effects=True, vmem_limit_bytes=62914560

time: 41.8 us -> 41.2 us (0.986)
  Pallas kernels: 40.9 us -> 40.4 us
    pallas_call x1, Pallas kernels: 40.9 us -> 40.4 us  [fused(): pl.pallas_call(functools.partial(kernel, n_row), out_shape=pltpu.VMEM((SU...]
where the time goes in v4:
time: 41.2 us; the launch traced here: 41 us
  Pallas kernels  40.4 us (98%)
  local copies, waits for them, and re-layouts  0.66 us (2%)
    pallas_call x1, Pallas kernels, fused(): pl.pallas_call(functools.partial(kernel, n_row), out_shape=pltpu.VMEM((SU...  40.4 us

profile of v4, /device:TPU:0, one launch (start us, length us, event | category | flops | bytes accessed | tf_op | source)
XLA Modules:
  0.0 41.0 jit_solution(9746506110369543443)
XLA Ops:
  0.0 40.4 %shard_map.46 = bf16[2,32,1024]{2,1,0:T(8,128)(2,1)S(1)} custom-call(bf16[4,2,2,2,16,1024]{5,4,3,2,1,0:T(8,128)(2,1)} %bitcast.3, bf16[1024,1280]{1,0:T(8,128)(2,1)} %wg_hbm.1, bf16[1024,1280]{1,0:T(8,128)(2,1)} %wu_hbm.1, bf16[1280,1024]{1,0:T(8,128)(2,1)} %wd_hbm.1), custom_call_target="tpu_custom_call" | custom-call | tf_op jit(solution)/shard_map/pallas_call | solution.py:350
  40.4 0.7 %copy.6 = bf16[64,1024]{1,0:T(8,128)(2,1)} copy(bf16[64,1024]{1,0:T(8,128)(2,1)S(1)} %bitcast.2) | data formatting | bytes 262144

commit v5 on v4

--- a/solution.py
+++ b/solution.py
@@ -10,10 +10,9 @@
 MESH = pl.DeviceIdType.MESH
 TILE = 256
 SUBS = 2
-MERGED = (6,)
 DIRECT = (6, 7)
 AHEAD = 3
-FLIGHT = 8
+FLIGHT = 6
 
 
 def activate(pre_gate, pre_up):
@@ -41,17 +40,13 @@
 
 
 ORDER = (
-    ("s1", 3), ("s2", 1), ("s1", 5), ("s2", 2), ("s2", 0), ("s2", 3), ("g1", 1), ("s1", 4),
-    ("g1", 2), ("s2", 5), ("g2", 1), ("g1", 0), ("g2", 2), ("g1", 3), ("s2", 4), ("g1", 5),
-    ("s1", 6), ("c1", 1), ("c2", 1), ("g2", 0), ("s1", 7), ("g2", 3), ("c1", 2), ("g1", 4),
-    ("c2", 2), ("s2", 6), ("g2", 5), ("c1", 0), ("c2", 0), ("s2", 7), ("c1", 3), ("g2", 4),
-    ("g1", 6), ("c2", 3), ("c1", 5), ("g1", 7), ("c2", 5), ("c1", 4), ("c2", 4), ("c1", 6),
-    ("c2", 7), ("c2", 6),
+    ("s1", 3), ("s2", 0), ("s2", 1), ("s1", 5), ("s2", 3), ("g1", 0), ("s2", 2), ("s1", 4),
+    ("g1", 1), ("s2", 5), ("g2", 0), ("g1", 2), ("g1", 3), ("g2", 1), ("s1", 6), ("s2", 4),
+    ("c1", 0), ("c2", 0), ("g2", 2), ("g1", 5), ("s1", 7), ("c1", 1), ("c2", 1), ("g2", 3),
+    ("g1", 4), ("s2", 6), ("c1", 2), ("g2", 5), ("c2", 2), ("s2", 7), ("c1", 3), ("g2", 4),
+    ("c2", 3), ("g1", 6), ("c1", 5), ("g1", 7), ("c2", 5), ("c1", 4), ("c2", 4), ("c1", 6),
+    ("c1", 7), ("c2", 7), ("c2", 6),
 )
-
-
-def schedule(chunks, ahead):
-    return ORDER, ORDER
 
 
 def kernel(
@@ -230,7 +225,7 @@
 
     def do_c1(j):
         if j in DIRECT:
-            do_own(range(j, chunks))
+            do_own([j])
             return
         arrived(hid.at[j, :, 0], recv2.at[j])
         rows = jnp.concatenate([hidden_rows(m, [j]) for m in range(2)], axis=1)
@@ -310,27 +305,17 @@
     for d in range(1, n_z - 2):
         relayed(d)
         relay(d + 1)
-    def run(order):
-        known = set()
-        for stage, j in order:
-            if stage == "c1" and stage not in known:
-                load_wd.wait()
-                relayed(n_z - 2)
-            if stage == "g1" and j in DIRECT and "diagonal" not in known:
-                known.add("diagonal")
-                pl.semaphore_wait(ready_diagonal, 1)
-            known.add(stage)
-            stages[stage](j)
-
-    orders = schedule(chunks, ahead)
-    if orders[0] == orders[1]:
-        run(orders[0])
-    else:
-        for c in range(2):
-            pl.when(core == c)(functools.partial(run, orders[c]))
-
-    if not DIRECT:
-        pl.semaphore_wait(ready_diagonal, 1)
+    known = set()
+    for stage, j in ORDER:
+        if stage == "c1" and stage not in known:
+            load_wd.wait()
+            relayed(n_z - 2)
+        if stage == "g1" and j in DIRECT and "diagonal" not in known:
+            known.add("diagonal")
+            pl.semaphore_wait(ready_diagonal, 1)
+        known.add(stage)
+        stages[stage](j)
+
     paired = chunks - len(DIRECT)
     waits = [(s1, 0), (s2, 1), (hid.at[:paired, :, 0, 0], 2), (hid.at[:paired, :, 0], 3), (c1s, 4), (c2s, 5)]
     if DIRECT:
@@ -363,7 +348,7 @@
             pltpu.VMEM((chunks, 2, each, width), bf16),
             pltpu.VMEM((chunks, 2, 2, 2, each, half), bf16),
             pltpu.VMEM((chunks, 2 * each, features), jnp.float32),
-            pltpu.VMEM((4 * SUBS * each, features), jnp.float32),
+            pltpu.VMEM((4 * each, features), jnp.float32),
             pltpu.VMEM((chunks, 2 * each, features), bf16),
             pltpu.VMEM((chunks, 2 * each, features), bf16),
             pltpu.VMEM((chunks - SUBS, 2 * each, features), bf16),
@@ -387,8 +372,8 @@
         width, features = w_down.shape
         fits = (
             n_col == 4
-            and 6 <= n_row <= 16
-            and n_row % 2 == 0
+            and n_row // 2 * SUBS == 1 + max(j for _, j in ORDER)
+            and n_row % 4 == 0
             and tokens.shape[0] % (n_row * 32 * SUBS) == 0
             and tokens.shape[0] <= 1024
             and width % TILE == 0

time: 41.2 us -> 40.9 us (level)
  no operation moved by 1% of the time
where the time goes in v5:
time: 40.9 us; the launch traced here: 40.7 us
  Pallas kernels  40.1 us (98%)
  local copies, waits for them, and re-layouts  0.66 us (2%)
    pallas_call x1, Pallas kernels, fused(): pl.pallas_call(functools.partial(kernel, n_row), out_shape=pltpu.VMEM((SU...  40.1 us

profile of v5, /device:TPU:0, one launch (start us, length us, event | category | flops | bytes accessed | tf_op | source)
XLA Modules:
  0.0 40.7 jit_solution(10264328843993180998)
XLA Ops:
  0.0 40.1 %shard_map.46 = bf16[2,32,1024]{2,1,0:T(8,128)(2,1)S(1)} custom-call(bf16[4,2,2,2,16,1024]{5,4,3,2,1,0:T(8,128)(2,1)} %bitcast.3, bf16[1024,1280]{1,0:T(8,128)(2,1)} %wg_hbm.1, bf16[1024,1280]{1,0:T(8,128)(2,1)} %wu_hbm.1, bf16[1280,1024]{1,0:T(8,128)(2,1)} %wd_hbm.1), custom_call_target="tpu_custom_call" | custom-call | tf_op jit(solution)/shard_map/pallas_call | solution.py:335
  40.1 0.7 %copy.6 = bf16[64,1024]{1,0:T(8,128)(2,1)} copy(bf16[64,1024]{1,0:T(8,128)(2,1)S(1)} %bitcast.2) | data formatting | bytes 262144

commit v6 on v5

--- a/solution.py
+++ b/solution.py
@@ -121,14 +121,14 @@
                 local(
                     w_hbm.at[:, pl.ds(m * half + low - k * half, high - low)],
                     w1.at[m, :, pl.ds(low, high - low)],
-                    3 + (2 * t + m) % FLIGHT,
+                    2 + (2 * t + m) % FLIGHT,
                 ).start()
 
     def wait_w1(m, t):
         columns = pl.ds(t * TILE, TILE)
-        local(wg_hbm.at[:, pl.ds(0, TILE)], w1.at[m, :, columns], 3 + (2 * t + m) % FLIGHT).wait()
-
-    load_wd = local(wd_hbm, wd, 2)
+        local(wg_hbm.at[:, pl.ds(0, TILE)], w1.at[m, :, columns], 2 + (2 * t + m) % FLIGHT).wait()
+
+    load_wd = local(wd_hbm, wd, 0)
     order_w1 = [(m, t) for t in range(n_tiles) for m in range(2)]
     load_tok(0).start()
     for m, t in order_w1[:FLIGHT]:
@@ -142,27 +142,27 @@
         return remote(s1.at[j, m], r1.at[j, m], 0, recv1.at[j], first_peer[m])
 
     def copy_s2(m, j):
-        return remote(s2.at[j, m], r2.at[j, m], 1, recv2.at[j], second_peer[m])
+        return remote(s2.at[j, m], r2.at[j, m], 0, recv2.at[j], second_peer[m])
 
     def copy_g1(m, j):
         ref = hid.at[j, m, first_at[m], second_at[m]]
-        return remote(ref, ref, 2, recv1.at[j], second_peer[m])
+        return remote(ref, ref, 0, recv1.at[j], second_peer[m])
 
     def copy_g2(m, j):
         ref = hid.at[j, m, first_at[m]]
-        return remote(ref, ref, 3, recv2.at[j], first_peer[m])
+        return remote(ref, ref, 0, recv2.at[j], first_peer[m])
 
     def copy_gd(m, j, peer):
         ref = hid.at[j, m, first_at[m], second_at[m]]
-        return remote(ref, ref, 6, recv3.at[2 * (j - remote_chunks) + m], peer)
+        return remote(ref, ref, 0, recv3.at[2 * (j - remote_chunks) + m], peer)
 
     def copy_c1(j):
-        return remote(c1s.at[j], c1r.at[j], 4, recv5.at[j], core_peer)
+        return remote(c1s.at[j], c1r.at[j], 1, recv5.at[j], core_peer)
 
     def copy_c2(j):
         k, sub = j // SUBS, j % SUBS
         slot = z - jnp.where(z > blocks[k], 1, 0)
-        return remote(c2s.at[j], c2r.at[sub, slot], 5, recv6.at[sub], z_peers[k])
+        return remote(c2s.at[j], c2r.at[sub, slot], 1, recv6.at[sub], z_peers[k])
 
     def arrived(ref, sem):
         remote(ref, ref, 0, sem, x_peer).wait_recv()
@@ -316,12 +316,10 @@
         known.add(stage)
         stages[stage](j)
 
-    paired = chunks - len(DIRECT)
-    waits = [(s1, 0), (s2, 1), (hid.at[:paired, :, 0, 0], 2), (hid.at[:paired, :, 0], 3), (c1s, 4), (c2s, 5)]
-    if DIRECT:
-        waits.append((hid.at[:3 * len(DIRECT), :, 0, 0], 6))
-    for ref, sem in waits:
-        left(ref, sem)
+    each = s2.shape[2]
+    pieces = chunks * 12 + (chunks - len(DIRECT)) * 6 + len(DIRECT) * 6
+    left(w1.at[:, :pieces * each // 4], 0)
+    left(wd.at[:(chunks + remote_chunks) * 2 * each], 1)
 
 
 def fused(n_row, tokens, w_gate, w_up, w_down):
@@ -353,7 +351,7 @@
             pltpu.VMEM((chunks, 2 * each, features), bf16),
             pltpu.VMEM((chunks - SUBS, 2 * each, features), bf16),
             pltpu.VMEM((SUBS, n_z - 1, 2 * each, features), bf16),
-            dma((3 + FLIGHT,)), dma((7,)),
+            dma((2 + FLIGHT,)), dma((2,)),
             dma((chunks,)), dma((chunks,)), dma((2 * SUBS,)), dma((chunks,)), dma((SUBS,)),
             pltpu.SemaphoreType.REGULAR((n_z - 2, 2)),
             pltpu.SemaphoreType.REGULAR,

time: 40.9 us -> 40.8 us (level)
  no operation moved by 1% of the time
where the time goes in v6:
time: 40.8 us; the launch traced here: 40.7 us
  Pallas kernels  40 us (98%)
  local copies, waits for them, and re-layouts  0.66 us (2%)
    pallas_call x1, Pallas kernels, fused(): pl.pallas_call(functools.partial(kernel, n_row), out_shape=pltpu.VMEM((SU...  40 us

profile of v6, /device:TPU:0, one launch (start us, length us, event | category | flops | bytes accessed | tf_op | source)
XLA Modules:
  0.0 40.7 jit_solution(7848199818841713845)
XLA Ops:
  0.0 40.0 %shard_map.46 = bf16[2,32,1024]{2,1,0:T(8,128)(2,1)S(1)} custom-call(bf16[4,2,2,2,16,1024]{5,4,3,2,1,0:T(8,128)(2,1)} %bitcast.3, bf16[1024,1280]{1,0:T(8,128)(2,1)} %wg_hbm.1, bf16[1024,1280]{1,0:T(8,128)(2,1)} %wu_hbm.1, bf16[1280,1024]{1,0:T(8,128)(2,1)} %wd_hbm.1), custom_call_target="tpu_custom_call" | custom-call | tf_op jit(solution)/shard_map/pallas_call | solution.py:333
  40.0 0.7 %copy.6 = bf16[64,1024]{1,0:T(8,128)(2,1)} copy(bf16[64,1024]{1,0:T(8,128)(2,1)S(1)} %bitcast.2) | data formatting | bytes 262144
